TPU v7x, 32 devices: a whole 2x2x4 slice. The times are simulated.
32 devices in a mesh: slab: 32 (over z, y, x, core).
Axes of the slice: x: 2, y: 2, z: 4, core: 2. Of those that a mesh axis runs over, the one named last changes fastest.
Arguments:
- start_vectors: float32 [2, 32, 256, 256], P(None, 'slab'), may hold values from -6 to 6
- levels: int32 [32, 256, 256], P('slab'), may hold values from 0 to 15
- energies: float32 [16], replicated, may hold values from -4 to 4
Outputs:
- cheb_field: float32 [2, 32, 256, 256], P(None, 'slab')
- lanczos_diag: float32 [2, 8], replicated
- lanczos_off: float32 [2, 7], replicated
- moments: float32 [2, 6], replicated
All inputs are finite; a program needn't handle non-finite values.
Results may differ from a plain program's by a relative error of at most 0.0001.
Values sent between devices are 32-bit elements; how exact they have to be, the bound alone decides.
A program may use at most 64 MiB of HBM per device.

v0:
```python
import jax
import jax.numpy as jnp
from jax import lax
from jax.sharding import PartitionSpec as P

LANCZOS = 8


def extended(value, sides, width):
    for axis, dim in sides:
        count, length = (lax.axis_size(axis), value.shape[dim])
        up = [(i, (i + 1) % count) for i in range(count)]
        down = [(j, i) for i, j in up]
        last = lax.slice_in_dim(value, length - width, length, axis=dim)
        initial = lax.slice_in_dim(value, 0, width, axis=dim)
        before = lax.ppermute(last, axis, up)
        after = lax.ppermute(initial, axis, down)
        value = jnp.concatenate([before, value, after], axis=dim)
    return value


def inner(first, second):
    return jnp.sum(first * second, axis=(1, 2, 3))


def expand(values):
    return values[:, None, None, None]


def in_plane(field):
    beside = jnp.roll(field, 1, 2) + jnp.roll(field, -1, 2)
    return beside + jnp.roll(field, 1, 3) + jnp.roll(field, -1, 3)


def hamiltonian(field, onsite):
    padded = extended(field, (("slab", 1),), 1)
    beside = padded[:, 2:] + padded[:, :-2] + in_plane(field)
    return onsite[None] * field - beside


def shards(start_vectors, levels, energies):
    level_ids = lax.broadcasted_iota(jnp.int32, (energies.shape[0], 1, 1, 1), 0)
    onsite = jnp.sum(
        jnp.where(levels[None] == level_ids, energies[:, None, None, None], 0.0), axis=0
    )
    vec_count = start_vectors.shape[0]
    norm0 = lax.psum(inner(start_vectors, start_vectors), "slab")
    vector = start_vectors / expand(jnp.sqrt(norm0))
    previous = jnp.zeros_like(vector)
    beta_prev = jnp.zeros((vec_count,), jnp.float32)
    alphas = []
    betas = []
    for step in range(LANCZOS):
        work = hamiltonian(vector, onsite) - expand(beta_prev) * previous
        alpha, square = lax.psum((inner(vector, work), inner(work, work)), "slab")
        alphas.append(alpha)
        if step < LANCZOS - 1:
            work = work - expand(alpha) * vector
            beta = jnp.sqrt(square - alpha * alpha)
            betas.append(beta)
            previous, vector, beta_prev = (vector, work / expand(beta), beta)
    diag = jnp.stack(alphas, axis=1)
    offd = jnp.stack(betas, axis=1)
    zero_col = jnp.zeros((vec_count, 1), jnp.float32)
    left = jnp.concatenate([zero_col, offd], axis=1)
    right = jnp.concatenate([offd, zero_col], axis=1)
    emin = jnp.min(diag - left - right, axis=1)
    emax = jnp.max(diag + left + right, axis=1)
    center = expand((emax + emin) * 0.5)
    half = expand(0.55 * (emax - emin))

    def scaled(field):
        return (hamiltonian(field, onsite) - center * field) / half

    def reduce_now(values):
        return lax.psum(values, "slab")

    term1 = scaled(start_vectors)
    term2 = 2.0 * scaled(term1) - start_vectors
    first = reduce_now(jnp.stack([inner(start_vectors, term1)], axis=0))
    second = reduce_now(jnp.stack([inner(start_vectors, term2), inner(term2, term2)], axis=0))
    term3 = 2.0 * scaled(term2) - term1
    third = reduce_now(
        jnp.stack([inner(start_vectors, term3), inner(term3, term2), inner(term3, term3)], axis=0)
    )
    sums = jnp.concatenate([first, second, third], axis=0)
    moments = (
        jnp.stack(
            [
                sums[0],
                sums[1],
                sums[3],
                2.0 * sums[2] - norm0,
                2.0 * sums[4] - sums[0],
                2.0 * sums[5] - norm0,
            ],
            axis=1,
        )
        / norm0[:, None]
    )
    return (term3, diag, offd, moments)


def solution(mesh):
    in_specs = (P(None, "slab", None, None), P("slab", None, None), P())
    out_specs = (P(None, "slab", None, None), P(), P(), P())
    return jax.shard_map(shards, mesh=mesh, in_specs=in_specs, out_specs=out_specs, check_vma=False)
```

profile of v0, /device:TPU:0, one launch (start us, length us, event | category | flops | bytes accessed | tf_op | source)
XLA Modules:
  0.0 580.4 jit_solution(17915568012401168470)
XLA Ops:
  1.9 41.9 %psum.133 = f32[2]{0:T(128)S(1)} all-reduce(f32[2]{0:T(128)S(1)} %multiply_reduce_fusion.20), channel_id=1, replica_groups=mesh['slab'=32] {'slab'}, use_global_device_ids=true, to_apply=%region_2.3 | all-reduce | flops 2 | bytes 16 | tf_op jit(solution)/shard_map/psum | solution.py:47
  59.4 44.5 %all-reduce.7 = (f32[2]{0:T(128)S(1)}, f32[2]{0:T(128)S(1)}) all-reduce(f32[2]{0:T(128)S(1)} %get-tuple-element.27, f32[2]{0:T(128)S(1)} %get-tuple-element.26), channel_id=1, replica_groups=mesh['slab'=32] {'slab'}, use_global_device_ids=true, to_apply=%region_6.7 | all-reduce | flops 4 | bytes 32 | tf_op jit(solution)/shard_map/psum | solution.py:55
  107.4 6.1 %collective-permute-done.4 = f32[2,1,256,256]{3,2,1,0:T(8,128)S(1)} collective-permute-done((f32[2,1,256,256]{3,2,1,0:T(8,128)S(1)}, f32[2,1,256,256]{3,2,1,0:T(8,128)S(1)}, u32[]{:S(2)}, u32[]{:S(2)}) %collective-permute-start.4) | collective-permute-done | bytes 524320 | tf_op jit(solution)/shard_map/ppermute | solution.py:17
  113.5 5.7 collective-permute-done.5
  121.0 39.1 %all-reduce.6 = (f32[2]{0:T(128)S(1)}, f32[2]{0:T(128)S(1)}) all-reduce(f32[2]{0:T(128)S(1)} %get-tuple-element.25, f32[2]{0:T(128)S(1)} %get-tuple-element.24), channel_id=1, replica_groups=mesh['slab'=32] {'slab'}, use_global_device_ids=true, to_apply=%region_10.11 | all-reduce | flops 4 | bytes 32 | tf_op jit(solution)/shard_map/psum | solution.py:55
  169.4 5.7 collective-permute-done.7
  177.0 39.4 %all-reduce.5 = (f32[2]{0:T(128)S(1)}, f32[2]{0:T(128)S(1)}) all-reduce(f32[2]{0:T(128)S(1)} %get-tuple-element.23, f32[2]{0:T(128)S(1)} %get-tuple-element.22), channel_id=1, replica_groups=mesh['slab'=32] {'slab'}, use_global_device_ids=true, to_apply=%region_14.15 | all-reduce | flops 4 | bytes 32 | tf_op jit(solution)/shard_map/psum | solution.py:55
  225.9 5.7 collective-permute-done.9
  233.4 38.9 %all-reduce.4 = (f32[2]{0:T(128)S(1)}, f32[2]{0:T(128)S(1)}) all-reduce(f32[2]{0:T(128)S(1)} %get-tuple-element.21, f32[2]{0:T(128)S(1)} %get-tuple-element.20), channel_id=1, replica_groups=mesh['slab'=32] {'slab'}, use_global_device_ids=true, to_apply=%region_18.19 | all-reduce | flops 4 | bytes 32 | tf_op jit(solution)/shard_map/psum | solution.py:55
  275.5 6.1 %collective-permute-done.10 = f32[2,1,256,256]{3,2,1,0:T(8,128)} collective-permute-done((f32[2,1,256,256]{3,2,1,0:T(8,128)S(1)}, f32[2,1,256,256]{3,2,1,0:T(8,128)}, u32[]{:S(2)}, u32[]{:S(2)}) %collective-permute-start.10) | collective-permute-done | bytes 524320 | tf_op jit(solution)/shard_map/ppermute | solution.py:17
  281.5 5.7 collective-permute-done.11
  289.8 39.5 %all-reduce.3 = (f32[2]{0:T(128)S(1)}, f32[2]{0:T(128)S(1)}) all-reduce(f32[2]{0:T(128)S(1)} %get-tuple-element.19, f32[2]{0:T(128)S(1)} %get-tuple-element.18), channel_id=1, replica_groups=mesh['slab'=32] {'slab'}, use_global_device_ids=true, to_apply=%region_22.23 | all-reduce | flops 4 | bytes 32 | tf_op jit(solution)/shard_map/psum | solution.py:55
  333.6 6.1 %collective-permute-done.12 = f32[2,1,256,256]{3,2,1,0:T(8,128)} collective-permute-done((f32[2,1,256,256]{3,2,1,0:T(8,128)S(1)}, f32[2,1,256,256]{3,2,1,0:T(8,128)}, u32[]{:S(2)}, u32[]{:S(2)}) %collective-permute-start.12) | collective-permute-done | bytes 524320 | tf_op jit(solution)/shard_map/ppermute | solution.py:17
  339.7 5.7 collective-permute-done.13
  347.9 38.6 %all-reduce.2 = (f32[2]{0:T(128)S(1)}, f32[2]{0:T(128)S(1)}) all-reduce(f32[2]{0:T(128)S(1)} %get-tuple-element.17, f32[2]{0:T(128)S(1)} %get-tuple-element.16), channel_id=1, replica_groups=mesh['slab'=32] {'slab'}, use_global_device_ids=true, to_apply=%region_26.27 | all-reduce | flops 4 | bytes 32 | tf_op jit(solution)/shard_map/psum | solution.py:55
  396.8 5.7 collective-permute-done.15
  405.1 39.6 %all-reduce.1 = (f32[2]{0:T(128)S(1)}, f32[2]{0:T(128)S(1)}) all-reduce(f32[2]{0:T(128)S(1)} %get-tuple-element.15, f32[2]{0:T(128)S(1)} %get-tuple-element.14), channel_id=1, replica_groups=mesh['slab'=32] {'slab'}, use_global_device_ids=true, to_apply=%region_30.31 | all-reduce | flops 4 | bytes 32 | tf_op jit(solution)/shard_map/psum | solution.py:55
  455.3 5.7 collective-permute-done.17
  462.8 38.6 %psum.148 = f32[2,1]{0,1:T(1,128)S(1)} all-reduce(f32[2,1]{0,1:T(1,128)S(1)} %bitcast.61), channel_id=1, replica_groups=mesh['slab'=32] {'slab'}, use_global_device_ids=true, to_apply=%region_32.33 | all-reduce | flops 2 | bytes 16 | tf_op jit(solution)/shard_map/psum | solution.py:55
  506.5 6.3 %collective-permute-done.18 = f32[2,1,256,256]{3,2,1,0:T(8,128)S(1)} collective-permute-done((f32[2,1,256,256]{3,2,1,0:T(8,128)S(1)}, f32[2,1,256,256]{3,2,1,0:T(8,128)S(1)}, u32[]{:S(2)}, u32[]{:S(2)}) %collective-permute-start.18) | collective-permute-done | bytes 524320 | tf_op jit(solution)/shard_map/ppermute | solution.py:17
  512.7 5.6 collective-permute-done.19
  519.8 5.8 collective-permute-done.20
  525.6 5.7 collective-permute-done.21
  532.7 46.4 %all-reduce = (f32[2,1]{0,1:T(1,128)S(1)}, f32[2,2]{1,0:T(2,128)S(1)}, f32[3,2]{1,0:T(4,128)S(1)}) all-reduce(f32[2,1]{0,1:T(1,128)S(1)} %bitcast.48, f32[2,2]{1,0:T(2,128)S(1)} %pad_maximum_fusion.1, f32[3,2]{1,0:T(4,128)S(1)} %pad_maximum_fusion), channel_id=1, replica_groups=mesh['slab'=32] {'slab'}, use_global_device_ids=true, to_apply=%region_36.37 | all-reduce | flops 12 | bytes 96 | tf_op jit(solution)/shard_map/psum | solution.py:76
  (172 shorter events, 91.4 us)
Async XLA Ops:
  0.6 43.2 %copy-start = (f32[2,1,256,256]{3,2,1,0:T(8,128)S(1)}, f32[2,1,256,256]{3,2,1,0:T(8,128)}, u32[]{:S(2)}) copy-start(f32[2,1,256,256]{3,2,1,0:T(8,128)} %param.3) | copy-start | bytes 1572868
  44.0 11.1 %collective-permute-start.2 = (f32[2,1,256,256]{3,2,1,0:T(8,128)S(1)}, f32[2,1,256,256]{3,2,1,0:T(8,128)S(1)}, u32[]{:S(2)}, u32[]{:S(2)}) collective-permute-start(f32[2,1,256,256]{3,2,1,0:T(8,128)S(1)} %broadcast_divide_fusion), channel_id=1, source_target_pairs={{1,0},{2,1},{3,2},{4,3},{5,4},{6,5},{7,6},{8,7},{9,8},{10,9},{11,1... | collective-permute-start | bytes 1572872 | tf_op jit(solution)/shard_map/ppermute | solution.py:17
  46.6 12.3 %collective-permute-start.3 = (f32[2,1,256,256]{3,2,1,0:T(8,128)S(1)}, f32[2,1,256,256]{3,2,1,0:T(8,128)S(1)}, u32[]{:S(2)}, u32[]{:S(2)}) collective-permute-start(f32[2,1,256,256]{3,2,1,0:T(8,128)S(1)} %broadcast_divide_fusion), channel_id=1, source_target_pairs={{0,1},{1,2},{2,3},{3,4},{4,5},{5,6},{6,7},{7,8},{8,9},{9,10},{10,1... | collective-permute-start | bytes 1572872 | tf_op jit(solution)/shard_map/ppermute | solution.py:16
  46.6 455.2 %collective-permute-start = (f32[2,1,256,256]{3,2,1,0:T(8,128)S(1)}, f32[2,1,256,256]{3,2,1,0:T(8,128)}, u32[]{:S(2)}, u32[]{:S(2)}) collective-permute-start(f32[2,1,256,256]{3,2,1,0:T(8,128)S(1)} %copy-done), channel_id=1, source_target_pairs={{1,0},{2,1},{3,2},{4,3},{5,4},{6,5},{7,6},{8,7},{9,8},{10,9},{11,1... | collective-permute-start | bytes 1572872 | tf_op jit(solution)/shard_map/ppermute | solution.py:17
  51.9 449.8 %collective-permute-start.1 = (f32[2,1,256,256]{3,2,1,0:T(8,128)S(1)}, f32[2,1,256,256]{3,2,1,0:T(8,128)}, u32[]{:S(2)}, u32[]{:S(2)}) collective-permute-start(f32[2,1,256,256]{3,2,1,0:T(8,128)S(1)} %copy-done), channel_id=1, source_target_pairs={{0,1},{1,2},{2,3},{3,4},{4,5},{5,6},{6,7},{7,8},{8,9},{9,10},{10,1... | collective-permute-start | bytes 1572872 | tf_op jit(solution)/shard_map/ppermute | solution.py:16
  104.1 9.4 %collective-permute-start.4 = (f32[2,1,256,256]{3,2,1,0:T(8,128)S(1)}, f32[2,1,256,256]{3,2,1,0:T(8,128)S(1)}, u32[]{:S(2)}, u32[]{:S(2)}) collective-permute-start(f32[2,1,256,256]{3,2,1,0:T(8,128)S(1)} %subtract_divide_fusion.6), channel_id=1, source_target_pairs={{1,0},{2,1},{3,2},{4,3},{5,4},{6,5},{7,6},{8,7},{9,8},{10,9},{11,1... | collective-permute-start | bytes 1572872 | tf_op jit(solution)/shard_map/ppermute | solution.py:17
  106.8 12.4 %collective-permute-start.5 = (f32[2,1,256,256]{3,2,1,0:T(8,128)S(1)}, f32[2,1,256,256]{3,2,1,0:T(8,128)}, u32[]{:S(2)}, u32[]{:S(2)}) collective-permute-start(f32[2,1,256,256]{3,2,1,0:T(8,128)S(1)} %subtract_divide_fusion.6), channel_id=1, source_target_pairs={{0,1},{1,2},{2,3},{3,4},{4,5},{5,6},{6,7},{7,8},{8,9},{9,10},{10,1... | collective-permute-start | bytes 1572872 | tf_op jit(solution)/shard_map/ppermute | solution.py:16
  160.2 9.2 %collective-permute-start.6 = (f32[2,1,256,256]{3,2,1,0:T(8,128)S(1)}, f32[2,1,256,256]{3,2,1,0:T(8,128)S(1)}, u32[]{:S(2)}, u32[]{:S(2)}) collective-permute-start(f32[2,1,256,256]{3,2,1,0:T(8,128)S(1)} %subtract_divide_fusion.5), channel_id=1, source_target_pairs={{1,0},{2,1},{3,2},{4,3},{5,4},{6,5},{7,6},{8,7},{9,8},{10,9},{11,1... | collective-permute-start | bytes 1572872 | tf_op jit(solution)/shard_map/ppermute | solution.py:17
  162.7 12.4 %collective-permute-start.7 = (f32[2,1,256,256]{3,2,1,0:T(8,128)S(1)}, f32[2,1,256,256]{3,2,1,0:T(8,128)}, u32[]{:S(2)}, u32[]{:S(2)}) collective-permute-start(f32[2,1,256,256]{3,2,1,0:T(8,128)S(1)} %subtract_divide_fusion.5), channel_id=1, source_target_pairs={{0,1},{1,2},{2,3},{3,4},{4,5},{5,6},{6,7},{7,8},{8,9},{9,10},{10,1... | collective-permute-start | bytes 1572872 | tf_op jit(solution)/shard_map/ppermute | solution.py:16
  216.5 9.4 %collective-permute-start.8 = (f32[2,1,256,256]{3,2,1,0:T(8,128)S(1)}, f32[2,1,256,256]{3,2,1,0:T(8,128)S(1)}, u32[]{:S(2)}, u32[]{:S(2)}) collective-permute-start(f32[2,1,256,256]{3,2,1,0:T(8,128)S(1)} %subtract_divide_fusion.4), channel_id=1, source_target_pairs={{1,0},{2,1},{3,2},{4,3},{5,4},{6,5},{7,6},{8,7},{9,8},{10,9},{11,1... | collective-permute-start | bytes 1572872 | tf_op jit(solution)/shard_map/ppermute | solution.py:17
  219.2 12.4 %collective-permute-start.9 = (f32[2,1,256,256]{3,2,1,0:T(8,128)S(1)}, f32[2,1,256,256]{3,2,1,0:T(8,128)}, u32[]{:S(2)}, u32[]{:S(2)}) collective-permute-start(f32[2,1,256,256]{3,2,1,0:T(8,128)S(1)} %subtract_divide_fusion.4), channel_id=1, source_target_pairs={{0,1},{1,2},{2,3},{3,4},{4,5},{5,6},{6,7},{7,8},{8,9},{9,10},{10,1... | collective-permute-start | bytes 1572872 | tf_op jit(solution)/shard_map/ppermute | solution.py:16
  272.4 9.1 %collective-permute-start.10 = (f32[2,1,256,256]{3,2,1,0:T(8,128)S(1)}, f32[2,1,256,256]{3,2,1,0:T(8,128)}, u32[]{:S(2)}, u32[]{:S(2)}) collective-permute-start(f32[2,1,256,256]{3,2,1,0:T(8,128)S(1)} %subtract_divide_fusion.3), channel_id=1, source_target_pairs={{1,0},{2,1},{3,2},{4,3},{5,4},{6,5},{7,6},{8,7},{9,8},{10,9},{11,1... | collective-permute-start | bytes 1572872 | tf_op jit(solution)/shard_map/ppermute | solution.py:17
  274.8 12.4 %collective-permute-start.11 = (f32[2,1,256,256]{3,2,1,0:T(8,128)S(1)}, f32[2,1,256,256]{3,2,1,0:T(8,128)}, u32[]{:S(2)}, u32[]{:S(2)}) collective-permute-start(f32[2,1,256,256]{3,2,1,0:T(8,128)S(1)} %subtract_divide_fusion.3), channel_id=1, source_target_pairs={{0,1},{1,2},{2,3},{3,4},{4,5},{5,6},{6,7},{7,8},{8,9},{9,10},{10,1... | collective-permute-start | bytes 1572872 | tf_op jit(solution)/shard_map/ppermute | solution.py:16
  330.5 9.2 %collective-permute-start.12 = (f32[2,1,256,256]{3,2,1,0:T(8,128)S(1)}, f32[2,1,256,256]{3,2,1,0:T(8,128)}, u32[]{:S(2)}, u32[]{:S(2)}) collective-permute-start(f32[2,1,256,256]{3,2,1,0:T(8,128)S(1)} %subtract_divide_fusion.2), channel_id=1, source_target_pairs={{1,0},{2,1},{3,2},{4,3},{5,4},{6,5},{7,6},{8,7},{9,8},{10,9},{11,1... | collective-permute-start | bytes 1572872 | tf_op jit(solution)/shard_map/ppermute | solution.py:17
  333.0 12.4 %collective-permute-start.13 = (f32[2,1,256,256]{3,2,1,0:T(8,128)S(1)}, f32[2,1,256,256]{3,2,1,0:T(8,128)}, u32[]{:S(2)}, u32[]{:S(2)}) collective-permute-start(f32[2,1,256,256]{3,2,1,0:T(8,128)S(1)} %subtract_divide_fusion.2), channel_id=1, source_target_pairs={{0,1},{1,2},{2,3},{3,4},{4,5},{5,6},{6,7},{7,8},{8,9},{9,10},{10,1... | collective-permute-start | bytes 1572872 | tf_op jit(solution)/shard_map/ppermute | solution.py:16
  387.7 9.1 %collective-permute-start.14 = (f32[2,1,256,256]{3,2,1,0:T(8,128)S(1)}, f32[2,1,256,256]{3,2,1,0:T(8,128)}, u32[]{:S(2)}, u32[]{:S(2)}) collective-permute-start(f32[2,1,256,256]{3,2,1,0:T(8,128)S(1)} %subtract_divide_fusion.1), channel_id=1, source_target_pairs={{1,0},{2,1},{3,2},{4,3},{5,4},{6,5},{7,6},{8,7},{9,8},{10,9},{11,1... | collective-permute-start | bytes 1572872 | tf_op jit(solution)/shard_map/ppermute | solution.py:17
  390.1 12.4 %collective-permute-start.15 = (f32[2,1,256,256]{3,2,1,0:T(8,128)S(1)}, f32[2,1,256,256]{3,2,1,0:T(8,128)}, u32[]{:S(2)}, u32[]{:S(2)}) collective-permute-start(f32[2,1,256,256]{3,2,1,0:T(8,128)S(1)} %subtract_divide_fusion.1), channel_id=1, source_target_pairs={{0,1},{1,2},{2,3},{3,4},{4,5},{5,6},{6,7},{7,8},{8,9},{9,10},{10,1... | collective-permute-start | bytes 1572872 | tf_op jit(solution)/shard_map/ppermute | solution.py:16
  445.9 9.4 %collective-permute-start.16 = (f32[2,1,256,256]{3,2,1,0:T(8,128)S(1)}, f32[2,1,256,256]{3,2,1,0:T(8,128)S(1)}, u32[]{:S(2)}, u32[]{:S(2)}) collective-permute-start(f32[2,1,256,256]{3,2,1,0:T(8,128)S(1)} %subtract_divide_fusion), channel_id=1, source_target_pairs={{1,0},{2,1},{3,2},{4,3},{5,4},{6,5},{7,6},{8,7},{9,8},{10,9},{11,1... | collective-permute-start | bytes 1572872 | tf_op jit(solution)/shard_map/ppermute | solution.py:17
  448.6 12.4 %collective-permute-start.17 = (f32[2,1,256,256]{3,2,1,0:T(8,128)S(1)}, f32[2,1,256,256]{3,2,1,0:T(8,128)}, u32[]{:S(2)}, u32[]{:S(2)}) collective-permute-start(f32[2,1,256,256]{3,2,1,0:T(8,128)S(1)} %subtract_divide_fusion), channel_id=1, source_target_pairs={{0,1},{1,2},{2,3},{3,4},{4,5},{5,6},{6,7},{7,8},{8,9},{9,10},{10,1... | collective-permute-start | bytes 1572872 | tf_op jit(solution)/shard_map/ppermute | solution.py:16
  461.0 40.8 %copy-start.1 = (f32[2,1,255,256]{3,2,1,0:T(8,128)S(1)}, f32[2,1,255,256]{3,2,1,0:T(8,128)}, u32[]{:S(2)}) copy-start(f32[2,1,255,256]{3,2,1,0:T(8,128)} %get-tuple-element.139) | copy-start | bytes 1566724
  503.7 9.1 %collective-permute-start.18 = (f32[2,1,256,256]{3,2,1,0:T(8,128)S(1)}, f32[2,1,256,256]{3,2,1,0:T(8,128)S(1)}, u32[]{:S(2)}, u32[]{:S(2)}) collective-permute-start(f32[2,1,256,256]{3,2,1,0:T(8,128)S(1)} %fusion.5), channel_id=1, source_target_pairs={{1,0},{2,1},{3,2},{4,3},{5,4},{6,5},{7,6},{8,7},{9,8},{10,9},{11,1... | collective-permute-start | bytes 1572872 | tf_op jit(solution)/shard_map/ppermute | solution.py:17
  506.0 12.3 %collective-permute-start.19 = (f32[2,1,256,256]{3,2,1,0:T(8,128)S(1)}, f32[2,1,256,256]{3,2,1,0:T(8,128)S(1)}, u32[]{:S(2)}, u32[]{:S(2)}) collective-permute-start(f32[2,1,256,256]{3,2,1,0:T(8,128)S(1)} %fusion.5), channel_id=1, source_target_pairs={{0,1},{1,2},{2,3},{3,4},{4,5},{5,6},{6,7},{7,8},{8,9},{9,10},{10,1... | collective-permute-start | bytes 1572872 | tf_op jit(solution)/shard_map/ppermute | solution.py:16
  518.8 6.8 %collective-permute-start.20 = (f32[2,1,256,256]{3,2,1,0:T(8,128)S(1)}, f32[2,1,256,256]{3,2,1,0:T(8,128)S(1)}, u32[]{:S(2)}, u32[]{:S(2)}) collective-permute-start(f32[2,1,256,256]{3,2,1,0:T(8,128)S(1)} %multiply_subtract_fusion.1), channel_id=1, source_target_pairs={{1,0},{2,1},{3,2},{4,3},{5,4},{6,5},{7,6},{8,7},{9,8},{10,9},{11,1... | collective-permute-start | bytes 1572872 | tf_op jit(solution)/shard_map/ppermute | solution.py:17
  518.9 12.4 %collective-permute-start.21 = (f32[2,1,256,256]{3,2,1,0:T(8,128)S(1)}, f32[2,1,256,256]{3,2,1,0:T(8,128)S(1)}, u32[]{:S(2)}, u32[]{:S(2)}) collective-permute-start(f32[2,1,256,256]{3,2,1,0:T(8,128)S(1)} %multiply_subtract_fusion.1), channel_id=1, source_target_pairs={{0,1},{1,2},{2,3},{3,4},{4,5},{5,6},{6,7},{7,8},{8,9},{9,10},{10,1... | collective-permute-start | bytes 1572872 | tf_op jit(solution)/shard_map/ppermute | solution.py:16
  (15 other events, 114.9 us)
where the time goes:
time: 582 us; the launch traced here: 580 us
  blocking collectives  406 us (70%)
  waiting for transfers between devices  106 us (18%)
  starting transfers between devices  28.7 us (5%)
  other arithmetic  26 us (4%)
  local copies, waits for them, and re-layouts  12.4 us (2%)
    psum x8, blocking collectives, shards(): alpha, square = lax.psum((inner(vector, work), inner(work, work)), 'slab')  318 us
    ppermute x11, waiting for transfers between devices, extended(): before = lax.ppermute(last, axis, up)  55 us
    ppermute x11, waiting for transfers between devices, extended(): after = lax.ppermute(initial, axis, down)  50.7 us
    psum x1, blocking collectives, reduce_now(): return lax.psum(values, 'slab')  46.4 us
    psum x1, blocking collectives, shards(): norm0 = lax.psum(inner(start_vectors, start_vectors), 'slab')  41.9 us
    ppermute x11, starting transfers between devices, extended(): after = lax.ppermute(initial, axis, down)  28.2 us
    reduce_sum x10, other arithmetic, inner(): return jnp.sum(first * second, axis=(1, 2, 3))  18.1 us
  transfers between devices with their start and end apart: 22, of which 19 were waited for; matrix products, arithmetic and copies ran while one was open for 5% of the time, Pallas kernels for 0%

commit v1 on v0

v1 whole, which is shorter than its diff:
```python
import functools

import jax
import jax.numpy as jnp
from jax import lax
from jax.experimental import pallas as pl
from jax.experimental.pallas import tpu as pltpu
from jax.sharding import PartitionSpec as P

LANCZOS = 8
HALF = LANCZOS // 2
GROUP = 8
GHOST = 8
RETURNED = 3


def phase_one(dots, half, sqrt):
    norm = dots[0]
    nu = [None] * len(dots)
    nu[0] = norm / norm
    nu[1] = dots[1] / norm
    for k in range(2, len(dots)):
        nu[k] = 2.0 * dots[k] / norm - nu[k % 2]
    top = len(nu) - 1
    row, before = list(nu), None
    diag, offd = [], []
    for k in range(half):
        if k == 0:
            alpha = row[1]
        else:
            alpha = (0.5 * row[k + 1] - offd[-1] * before[k]) / row[k]
        diag.append(alpha)
        new = [None] * len(nu)
        for l in range(k + 1, top - k):
            new[l] = 0.5 * (row[l + 1] + row[l - 1]) - alpha * row[l]
            if k:
                new[l] = new[l] - offd[-1] * before[l]
        beta = sqrt(new[k + 1] / (row[k] if k == 0 else 2.0 * row[k]))
        offd.append(beta)
        inv = 1.0 / beta
        before, row = row, [None if x is None else x * inv for x in new]
    zero = nu[0] * 0.0
    scale = 1.0 / sqrt(norm)
    vectors = [[scale] + [zero] * half]
    for k in range(half):
        now = vectors[-1]
        inv = 1.0 / offd[k]
        shifted = [zero] * (half + 1)
        for l in range(k + 1):
            if l == 0:
                shifted[1] = shifted[1] + now[0]
            else:
                shifted[l + 1] = shifted[l + 1] + 0.5 * now[l]
                shifted[l - 1] = shifted[l - 1] + 0.5 * now[l]
        new = [shifted[l] - diag[k] * now[l] for l in range(half + 1)]
        if k:
            new = [x - offd[k - 1] * y for x, y in zip(new, vectors[-2])]
        vectors.append([x * inv for x in new])
    return nu, diag, offd, vectors


def phase_two(dots, diag, offd, half, sqrt):
    count = len(dots)
    gram = {}
    for k, value in enumerate(dots):
        gram[(half + k // 2, half + (k + 1) // 2)] = value
    zero = dots[0] * 0.0
    one = zero + 1.0
    for k in range(half):
        gram[(k, half)] = zero
        gram[(k, half - 1)] = one if k == half - 1 else zero
    guess_a, guess_b = diag[half - 1], offd[half - 1]
    inv = 1.0 / guess_b

    def entry(i, j):
        if (i, j) in gram:
            return gram[(i, j)]
        if j > half and i < half and (j - half) < (half - i) + 1:
            value = zero
        elif i >= half:
            value = entry(i + 1, j - 1) + entry(i - 1, j - 1) - entry(i, j - 2)
        else:
            value = (offd[i] * inv) * entry(i + 1, j - 1) - entry(i, j - 2)
            if i != half - 1:
                value = value + ((diag[i] - guess_a) * inv) * entry(i, j - 1)
            if i > 0:
                value = value + (offd[i - 1] * inv) * entry(i - 1, j - 1)
        gram[(i, j)] = value
        return value

    top = half + count - 1
    row = {l: entry(half, l) for l in range(half, top + 1)}
    before = {l: entry(half - 1, l) for l in range(half, top)}
    diag, offd = list(diag), list(offd)
    for k in range(half, 2 * half):
        if k == half:
            alpha = guess_a + guess_b * row[k + 1] / row[k]
        else:
            alpha = guess_a + (guess_b * row[k + 1] - offd[k - 1] * before[k]) / row[k]
        diag.append(alpha)
        if k == 2 * half - 1:
            break
        new = {}
        for l in range(k + 1, top - (k - half)):
            new[l] = guess_b * (row[l + 1] + row[l - 1]) + (guess_a - alpha) * row[l] - offd[k - 1] * before[l]
        beta = sqrt(new[k + 1] * guess_b / row[k])
        offd.append(beta)
        inv_b = 1.0 / beta
        before, row = row, {l: x * inv_b for l, x in new.items()}
    return diag, offd


def chebyshev(diag, offd, nu, centre, width):
    left = [None] + offd
    right = offd + [None]
    low, high = None, None
    for a, b, c in zip(diag, left, right):
        reach = b if c is None else c if b is None else b + c
        low = a - reach if low is None else jnp.minimum(low, a - reach)
        high = a + reach if high is None else jnp.maximum(high, a + reach)
    inv = 1.0 / (0.55 * (high - low))
    al = width * inv
    be = (centre - 0.5 * (high + low)) * inv
    p, q, r = 2.0 * be * be + al * al - 1.0, 4.0 * al * be, al * al
    first = [be, al]
    second = [p, q, r]
    third = [2.0 * be * p + al * q - be, 2.0 * be * q + al * (2.0 * p + r) - al, 2.0 * be * r + al * q, al * r]

    def dot(f, g):
        total = None
        for i, x in enumerate(f):
            for j, y in enumerate(g):
                term = (x * y) * (0.5 * (nu[i + j] + nu[abs(i - j)]))
                total = term if total is None else total + term
        return total

    start = [nu[0]]
    m1 = dot(start, first)
    moments = [
        m1,
        dot(start, second),
        dot(start, third),
        2.0 * dot(second, second) - 1.0,
        2.0 * dot(third, second) - m1,
        2.0 * dot(third, third) - 1.0,
    ]
    return third, moments


def kernel(
    count, energies, start, levels, cheb, diag_out, offd_out, moments_out,
    own, own_levels, field, halo, onsite, level, back, part, part_far, mine,
    load_sem, vec_sem, level_sem, halo_send, halo_recv, back_send, back_recv, red_send, red_recv,
):
    me = lax.axis_index("slab")
    member = lax.rem(me, GROUP)
    group = me // GROUP
    base = me - member
    groups = count // GROUP
    vecs, _, height, lanes = start.shape
    rows = height // GROUP
    deep = rows + 2 * GHOST
    mesh_id = pl.DeviceIdType.MESH
    ahead = lax.rem(me + GROUP, count)
    behind = lax.rem(me + count - GROUP, count)

    loads = [
        pltpu.make_async_copy(start.at[:, 0], own, load_sem.at[0]),
        pltpu.make_async_copy(levels.at[0], own_levels, load_sem.at[1]),
    ]
    for copy in loads:
        copy.start()

    def peer(i):
        return base + lax.rem(member + i, GROUP)

    def far(i):
        return lax.rem(me + i * GROUP, count)

    barrier = pltpu.get_barrier_semaphore()

    def greet(i, carry):
        pl.semaphore_signal(barrier, inc=1, device_id=(peer(i),), device_id_type=mesh_id)
        return carry

    def greet_far(i, carry):
        pl.semaphore_signal(barrier, inc=1, device_id=(far(i),), device_id_type=mesh_id)
        return carry

    lax.fori_loop(1, GROUP, greet, 0)
    lax.fori_loop(1, groups, greet_far, 0)
    pl.semaphore_wait(barrier, GROUP - 1 + groups - 1)

    def pieces(i):
        mid = pl.multiple_of(i * rows, 8)
        top = pl.multiple_of(lax.rem(i * rows + height - GHOST, height), 8)
        low = pl.multiple_of(lax.rem(i * rows + rows, height), 8)
        return ((mid, GHOST, rows), (top, 0, GHOST), (low, GHOST + rows, GHOST))

    def vec_refs(i):
        return [
            (own.at[:, pl.ds(at, size)], field.at[0, :, member, pl.ds(to, size)])
            for at, to, size in pieces(i)
        ]

    def level_refs(i):
        return [
            (own_levels.at[pl.ds(at, size)], level.at[member, pl.ds(to, size)])
            for at, to, size in pieces(i)
        ]

    def scatter(refs, sems):
        def body(i, carry):
            to = lax.rem(member + i, GROUP)
            for src, dst in refs(to):
                pltpu.make_async_remote_copy(
                    src_ref=src, dst_ref=dst, send_sem=sems.at[0], recv_sem=sems.at[1],
                    device_id=(base + to,), device_id_type=mesh_id,
                ).start()
            return carry

        lax.fori_loop(1, GROUP, body, 0)
        for src, dst in refs(member):
            pltpu.make_async_copy(src, dst, sems.at[1]).start()

    def drain(ref, sem):
        pltpu.make_async_copy(ref, ref, sem).wait()

    loads[0].wait()
    scatter(vec_refs, vec_sem)
    loads[1].wait()
    scatter(level_refs, level_sem)

    values = [energies[i] for i in range(energies.shape[0])]
    mean = sum(values[1:], values[0]) * (1.0 / len(values))
    spread = [(x - mean) * (x - mean) for x in values]
    spread = sum(spread[1:], spread[0]) * (1.0 / len(values))
    width = 2.0 * jnp.sqrt(jnp.full((1, lanes), spread + 6.0, jnp.float32))
    inv_width = 1.0 / width

    def halo_copies(slot, at):
        return [
            pltpu.make_async_remote_copy(
                src_ref=field.at[slot, :, plane], dst_ref=halo.at[at, side],
                send_sem=halo_send.at[at, side], recv_sem=halo_recv.at[at, side],
                device_id=(to,), device_id_type=mesh_id,
            )
            for plane, side, to in ((0, 1, behind), (GROUP - 1, 0, ahead))
        ]

    def give_back(k):
        def refs(i):
            return (
                field.at[k, :, i, pl.ds(GHOST, rows)],
                back.at[k - 1, :, pl.ds(pl.multiple_of(member * rows, 8), rows)],
            )

        def body(i, carry):
            to = lax.rem(member + i, GROUP)
            src, dst = refs(to)
            pltpu.make_async_remote_copy(
                src_ref=src, dst_ref=dst, send_sem=back_send.at[k - 1], recv_sem=back_recv.at[k - 1],
                device_id=(base + to,), device_id_type=mesh_id,
            ).start()
            return carry

        lax.fori_loop(1, GROUP, body, 0)
        src, dst = refs(member)
        pltpu.make_async_copy(src, dst, back_recv.at[k - 1]).start()

    def tile_sum(x):
        x = x[GHOST : GHOST + rows]
        total = x[0:8]
        for i in range(8, rows, 8):
            total = total + x[i : i + 8]
        return total

    def step(source, target, before, at, combine, extra=False):
        nothing = jnp.zeros((8, lanes), jnp.float32)

        def plane(m, below, above, sums):
            sums = list(sums)
            for v in range(vecs):
                here = field[source, v, m]
                near = pltpu.roll(here, 1, 0) + pltpu.roll(here, deep - 1, 0)
                near = near + pltpu.roll(here, 1, 1) + pltpu.roll(here, lanes - 1, 1)
                near = near + below(v) + above(v)
                applied = onsite[m] * here - inv_width * near
                new = combine(v, applied, here, None if before is None else field[before, v, m])
                if target is not None:
                    field[target, v, m] = new
                sums[3 * v] = sums[3 * v] + tile_sum(here * new)
                sums[3 * v + 1] = sums[3 * v + 1] + tile_sum(new * new)
                if extra:
                    sums[3 * v + 2] = sums[3 * v + 2] + tile_sum(here * here)
            return tuple(sums)

        sums = (nothing,) * (3 * vecs)
        sums = plane(0, lambda v: halo[at, 0, v], lambda v: field[source, v, 1], sums)
        sums = plane(
            GROUP - 1, lambda v: field[source, v, GROUP - 2], lambda v: halo[at, 1, v], sums
        )
        sent = []
        if target is not None:
            sent = halo_copies(target, at + 1)
            for copy in sent:
                copy.start()
        sums = lax.fori_loop(
            1,
            GROUP - 1,
            lambda m, carry: plane(
                m, lambda v: field[source, v, m - 1], lambda v: field[source, v, m + 1], carry
            ),
            sums,
        )
        return sums, sent

    lane = lax.broadcasted_iota(jnp.int32, (8, 128), 1)
    line = lax.broadcasted_iota(jnp.int32, (8, 128), 0)

    def reduce_all(dots, turn):
        tile = jnp.zeros((8, 128), jnp.float32)
        for d, per_vec in enumerate(dots):
            for v, value in enumerate(per_vec):
                whole = jnp.sum(jnp.sum(value, axis=0, keepdims=True), axis=1, keepdims=True)
                tile = jnp.where((lane == d) & (line == v), whole, tile)
        for leg, (slots, index, size, target) in enumerate(
            ((part.at[turn], member, GROUP, peer), (part_far.at[turn], group, groups, far))
        ):
            mine[turn, leg] = tile
            slots[index] = tile

            def body(i, carry):
                pltpu.make_async_remote_copy(
                    src_ref=mine.at[turn, leg], dst_ref=slots.at[index],
                    send_sem=red_send.at[turn, leg], recv_sem=red_recv.at[turn, leg],
                    device_id=(target(i),), device_id_type=mesh_id,
                ).start()
                return carry

            lax.fori_loop(1, size, body, 0)
            drain(slots.at[pl.ds(0, size - 1)], red_recv.at[turn, leg])
            tile = slots[0]
            for i in range(1, size):
                tile = tile + slots[i]
        return [
            jnp.broadcast_to(tile[0:vecs, d : d + 1], (vecs, lanes)) for d in range(len(dots))
        ]

    drain(field.at[0], vec_sem.at[1])
    sent = [halo_copies(0, 0)]
    for copy in sent[0]:
        copy.start()
    drain(level, level_sem.at[1])

    def look_up(m, carry):
        ids = level[m]
        energy = jnp.full(ids.shape, values[0] - mean, jnp.float32)
        for i in range(1, len(values)):
            energy = jnp.where(ids == i, values[i] - mean, energy)
        onsite[m] = energy * inv_width
        return carry

    lax.fori_loop(0, GROUP, look_up, 0)

    def arrive(copies):
        for copy in copies:
            copy.wait_recv()

    dots = [None]
    for k in range(HALF):
        arrive(sent[k])
        if k == 0:
            rule = lambda v, applied, here, old: applied
        else:
            rule = lambda v, applied, here, old: 2.0 * applied - old
        sums, copies = step(k, k + 1, k - 1 if k else None, k, rule, extra=k == 0)
        sent.append(copies)
        if k == 0:
            dots[0] = [sums[3 * v + 2] for v in range(vecs)]
        dots.append([sums[3 * v] for v in range(vecs)])
        dots.append([sums[3 * v + 1] for v in range(vecs)])
        if k + 1 <= RETURNED:
            give_back(k + 1)

    totals = reduce_all(dots, 0)
    nu, diag, offd, vectors = phase_one(totals, HALF, jnp.sqrt)
    arrive(sent[HALF])
    old_at, new_at = HALF + 1, HALF + 2

    def mix(coefficients, v, read):
        total = coefficients[0][v : v + 1] * read(0)
        for k in range(1, len(coefficients)):
            total = total + coefficients[k][v : v + 1] * read(k)
        return total

    old_mix, new_mix = vectors[HALF - 1][:HALF], vectors[HALF]
    for side in range(2):
        for v in range(vecs):
            halo[HALF, side, v] = mix(new_mix, v, lambda k: halo[k, side, v])

    def restart(m, sums):
        sums = list(sums)
        for v in range(vecs):
            field[old_at, v, m] = mix(old_mix, v, lambda k: field[k, v, m])
            new = mix(new_mix, v, lambda k: field[k, v, m])
            field[new_at, v, m] = new
            sums[v] = sums[v] + tile_sum(new * new)
        return tuple(sums)

    sums = lax.fori_loop(0, GROUP, restart, (jnp.zeros((8, lanes), jnp.float32),) * vecs)
    dots = [list(sums)]
    gain = 1.0 / offd[HALF - 1]
    shift = diag[HALF - 1]

    def rule(v, applied, here, old):
        return gain[v : v + 1] * (applied - shift[v : v + 1] * here) - old

    for k in range(HALF):
        at = HALF + k
        if k:
            arrive(sent[at])
        last = k == HALF - 1
        sums, copies = step(new_at + k, None if last else new_at + k + 1, new_at + k - 1, at, rule)
        sent.append(copies)
        dots.append([sums[3 * v] for v in range(vecs)])
        if not last:
            dots.append([sums[3 * v + 1] for v in range(vecs)])

    totals = reduce_all(dots, 1)
    diag, offd = phase_two(totals, diag, offd, HALF, jnp.sqrt)
    diag = [width * a + mean for a in diag]
    offd = [width * b for b in offd]
    third, moments = chebyshev(diag, offd, nu, mean, width)

    for k in range(RETURNED):
        drain(back.at[k], back_recv.at[k])
    for v in range(vecs):
        cheb[v, 0] = mix(third, v, lambda k: own[v] if k == 0 else back[k - 1, v])

    for ref, items in ((diag_out, diag), (offd_out, offd), (moments_out, moments)):
        at = lax.broadcasted_iota(jnp.int32, ref.shape, 1)
        value = jnp.zeros(ref.shape, jnp.float32)
        for i, item in enumerate(items):
            value = jnp.where(at == i, item[:, : ref.shape[1]], value)
        ref[...] = value

    for copies in sent:
        for copy in copies:
            copy.wait_send()
    drain(field.at[0, :, pl.ds(0, GROUP - 1)], vec_sem.at[0])
    drain(level.at[pl.ds(0, GROUP - 1)], level_sem.at[0])
    for k in range(RETURNED):
        drain(field.at[k + 1, :, pl.ds(0, GROUP - 1), pl.ds(GHOST, rows)], back_send.at[k])
    for turn in range(2):
        drain(part.at[turn, pl.ds(0, GROUP - 1)], red_send.at[turn, 0])
        drain(part_far.at[turn, pl.ds(0, groups - 1)], red_send.at[turn, 1])


def shards(count, start_vectors, levels, energies):
    vecs, _, height, lanes = start_vectors.shape
    groups = count // GROUP
    deep = height // GROUP + 2 * GHOST
    f32 = jnp.float32
    vmem = pl.BlockSpec(memory_space=pltpu.VMEM)
    anywhere = pl.BlockSpec(memory_space=pl.ANY)
    dma = pltpu.SemaphoreType.DMA
    return pl.pallas_call(
        functools.partial(kernel, count),
        out_shape=(
            jax.ShapeDtypeStruct(start_vectors.shape, f32),
            jax.ShapeDtypeStruct((vecs, LANCZOS), f32),
            jax.ShapeDtypeStruct((vecs, LANCZOS - 1), f32),
            jax.ShapeDtypeStruct((vecs, 6), f32),
        ),
        in_specs=[pl.BlockSpec(memory_space=pltpu.SMEM), anywhere, anywhere],
        out_specs=(vmem,) * 4,
        scratch_shapes=[
            pltpu.VMEM((vecs, height, lanes), f32),
            pltpu.VMEM((height, lanes), jnp.int32),
            pltpu.VMEM((LANCZOS + 2, vecs, GROUP, deep, lanes), f32),
            pltpu.VMEM((LANCZOS, 2, vecs, deep, lanes), f32),
            pltpu.VMEM((GROUP, deep, lanes), f32),
            pltpu.VMEM((GROUP, deep, lanes), jnp.int32),
            pltpu.VMEM((RETURNED, vecs, height, lanes), f32),
            pltpu.VMEM((2, GROUP, 8, 128), f32),
            pltpu.VMEM((2, groups, 8, 128), f32),
            pltpu.VMEM((2, 2, 8, 128), f32),
            dma((2,)),
            dma((2,)),
            dma((2,)),
            dma((LANCZOS, 2)),
            dma((LANCZOS, 2)),
            dma((RETURNED,)),
            dma((RETURNED,)),
            dma((2, 2)),
            dma((2, 2)),
        ],
        compiler_params=pltpu.CompilerParams(
            collective_id=0, has_side_effects=True, vmem_limit_bytes=48 * 1024 * 1024
        ),
    )(energies, start_vectors, levels)


def solution(mesh):
    in_specs = (P(None, "slab", None, None), P("slab", None, None), P())
    out_specs = (P(None, "slab", None, None), P(), P(), P())
    return jax.shard_map(
        functools.partial(shards, mesh.shape["slab"]),
        mesh=mesh, in_specs=in_specs, out_specs=out_specs, check_vma=False,
    )
```

time: 582 us -> 82.6 us (0.14)
  blocking collectives: 406 us -> 0 us
  waiting for transfers between devices: 106 us -> 0 us
  Pallas kernels: 0 us -> 76.6 us
  starting transfers between devices: 28.7 us -> 0 us
  other arithmetic: 26 us -> 0 us
  local copies, waits for them, and re-layouts: 12.4 us -> 5.12 us
    psum x10 -> x0, blocking collectives: 406 us -> none  [the longest x8 318 us: shards(): alpha, square = lax.psum((inner(vector, work), inner(work, work)), 'slab')]
    ppermute x22 -> x0, waiting for transfers between devices: 106 us -> none  [the longest x11 55 us: extended(): before = lax.ppermute(last, axis, up)]
    pallas_call x0 -> x1, Pallas kernels: none -> 76.6 us  [shards(): pl.pallas_call(functools.partial(kernel, count), out_shape=(jax.ShapeDtyp...]
    ppermute x22 -> x0, starting transfers between devices: 28.7 us -> none  [the longest x11 28.2 us: extended(): after = lax.ppermute(initial, axis, down)]
    reduce_sum x11 -> x0, other arithmetic: 18.6 us -> none  [the longest x10 18.1 us: inner(): return jnp.sum(first * second, axis=(1, 2, 3))]
    slice x44 -> x0, local copies, waits for them, and re-layouts: 9.25 us -> none  [the longest x22 7.4 us: in_plane(): return beside + jnp.roll(field, 1, 3) + jnp.roll(field, -1, 3)]
    div x10 -> x0, other arithmetic: 6.74 us -> none  [the longest x7 4.1 us: shards(): previous, vector, beta_prev = (vector, work / expand(beta), beta)]
  transfers between devices with their start and end apart: 22 -> 0, of which waited for: 19 -> 0; matrix products, arithmetic and copies ran while one was open for 5% -> 0% of each run, Pallas kernels for 0% -> 0%
where the time goes in v1:
time: 82.6 us; the launch traced here: 82.4 us
  Pallas kernels  76.6 us (93%)
  local copies, waits for them, and re-layouts  5.12 us (6%)
    pallas_call x1, Pallas kernels, shards(): pl.pallas_call(functools.partial(kernel, count), out_shape=(jax.ShapeDtyp...  76.6 us
    unnamed x10, local copies, waits for them, and re-layouts  5.12 us

profile of v1, /device:TPU:0, one launch (start us, length us, event | category | flops | bytes accessed | tf_op | source)
XLA Modules:
  0.0 82.4 jit_solution(10660019759812412958)
XLA Ops:
  0.6 0.0 copy-start
  0.6 1.0 %copy-done = f32[2,1,256,256]{3,2,1,0:T(8,128)S(1)} copy-done((f32[2,1,256,256]{3,2,1,0:T(8,128)S(1)}, f32[2,1,256,256]{3,2,1,0:T(8,128)}, u32[]{:S(2)}) %copy-start) | copy-done | bytes 524312
  1.7 0.0 copy-start.1
  1.7 0.9 %copy-done.1 = s32[1,256,256]{2,1,0:T(8,128)S(1)} copy-done((s32[1,256,256]{2,1,0:T(8,128)S(1)}, s32[1,256,256]{2,1,0:T(8,128)}, u32[]{:S(2)}) %copy-start.1) | copy-done | bytes 262168
  2.6 0.0 copy-start.2
  2.6 0.7 copy-done.2
  3.3 76.6 %shard_map.66 = (f32[2,1,256,256]{3,2,1,0:T(8,128)S(1)}, f32[2,8]{1,0:T(2,128)S(1)}, f32[2,7]{1,0:T(2,128)S(1)}, f32[2,6]{1,0:T(2,128)S(1)}) custom-call(f32[16]{0:T(128)S(1)} %copy-done.2, f32[2,1,256,256]{3,2,1,0:T(8,128)S(1)} %copy-done, s32[1,256,256]{2,1,0:T(8,128)S(1)} %copy-done.1), custom_call_target="tpu_custom_call" | custom-call | tf_op jit(solution)/shard_map/pallas_call | solution.py:468
  79.9 0.8 copy.11
  80.7 0.6 copy.12
  81.3 0.6 copy.13
  81.8 0.6 copy.14
Async XLA Ops:
  0.6 1.0 %copy-start = (f32[2,1,256,256]{3,2,1,0:T(8,128)S(1)}, f32[2,1,256,256]{3,2,1,0:T(8,128)}, u32[]{:S(2)}) copy-start(f32[2,1,256,256]{3,2,1,0:T(8,128)} %start.1) | copy-start | bytes 1572868
  1.7 0.9 %copy-start.1 = (s32[1,256,256]{2,1,0:T(8,128)S(1)}, s32[1,256,256]{2,1,0:T(8,128)}, u32[]{:S(2)}) copy-start(s32[1,256,256]{2,1,0:T(8,128)} %levels.1) | copy-start | bytes 786436
  2.6 0.7 copy-start.2

commit v2 on v1

--- a/solution.py
+++ b/solution.py
@@ -158,7 +158,8 @@
     base = me - member
     groups = count // GROUP
     vecs, _, height, lanes = start.shape
-    rows = height // GROUP
+    my_vec, block = lax.rem(member, vecs), member // vecs
+    rows = height // (GROUP // vecs)
     deep = rows + 2 * GHOST
     mesh_id = pl.DeviceIdType.MESH
     ahead = lax.rem(me + GROUP, count)
@@ -192,6 +193,7 @@
     pl.semaphore_wait(barrier, GROUP - 1 + groups - 1)
 
     def pieces(i):
+        i = i // vecs
         mid = pl.multiple_of(i * rows, 8)
         top = pl.multiple_of(lax.rem(i * rows + height - GHOST, height), 8)
         low = pl.multiple_of(lax.rem(i * rows + rows, height), 8)
@@ -199,7 +201,7 @@
 
     def vec_refs(i):
         return [
-            (own.at[:, pl.ds(at, size)], field.at[0, :, member, pl.ds(to, size)])
+            (own.at[lax.rem(i, vecs), pl.ds(at, size)], field.at[0, member, pl.ds(to, size)])
             for at, to, size in pieces(i)
         ]
 
@@ -241,7 +243,7 @@
     def halo_copies(slot, at):
         return [
             pltpu.make_async_remote_copy(
-                src_ref=field.at[slot, :, plane], dst_ref=halo.at[at, side],
+                src_ref=field.at[slot, plane], dst_ref=halo.at[at, side],
                 send_sem=halo_send.at[at, side], recv_sem=halo_recv.at[at, side],
                 device_id=(to,), device_id_type=mesh_id,
             )
@@ -251,8 +253,8 @@
     def give_back(k):
         def refs(i):
             return (
-                field.at[k, :, i, pl.ds(GHOST, rows)],
-                back.at[k - 1, :, pl.ds(pl.multiple_of(member * rows, 8), rows)],
+                field.at[k, i, pl.ds(GHOST, rows)],
+                back.at[k - 1, my_vec, pl.ds(pl.multiple_of(block * rows, 8), rows)],
             )
 
         def body(i, carry):
@@ -280,26 +282,23 @@
 
         def plane(m, below, above, sums):
             sums = list(sums)
-            for v in range(vecs):
-                here = field[source, v, m]
-                near = pltpu.roll(here, 1, 0) + pltpu.roll(here, deep - 1, 0)
-                near = near + pltpu.roll(here, 1, 1) + pltpu.roll(here, lanes - 1, 1)
-                near = near + below(v) + above(v)
-                applied = onsite[m] * here - inv_width * near
-                new = combine(v, applied, here, None if before is None else field[before, v, m])
-                if target is not None:
-                    field[target, v, m] = new
-                sums[3 * v] = sums[3 * v] + tile_sum(here * new)
-                sums[3 * v + 1] = sums[3 * v + 1] + tile_sum(new * new)
-                if extra:
-                    sums[3 * v + 2] = sums[3 * v + 2] + tile_sum(here * here)
+            here = field[source, m]
+            near = pltpu.roll(here, 1, 0) + pltpu.roll(here, deep - 1, 0)
+            near = near + pltpu.roll(here, 1, 1) + pltpu.roll(here, lanes - 1, 1)
+            near = near + below() + above()
+            applied = onsite[m] * here - inv_width * near
+            new = combine(applied, here, None if before is None else field[before, m])
+            if target is not None:
+                field[target, m] = new
+            sums[0] = sums[0] + tile_sum(here * new)
+            sums[1] = sums[1] + tile_sum(new * new)
+            if extra:
+                sums[2] = sums[2] + tile_sum(here * here)
             return tuple(sums)
 
-        sums = (nothing,) * (3 * vecs)
-        sums = plane(0, lambda v: halo[at, 0, v], lambda v: field[source, v, 1], sums)
-        sums = plane(
-            GROUP - 1, lambda v: field[source, v, GROUP - 2], lambda v: halo[at, 1, v], sums
-        )
+        sums = (nothing,) * 3
+        sums = plane(0, lambda: halo[at, 0], lambda: field[source, 1], sums)
+        sums = plane(GROUP - 1, lambda: field[source, GROUP - 2], lambda: halo[at, 1], sums)
         sent = []
         if target is not None:
             sent = halo_copies(target, at + 1)
@@ -309,7 +308,7 @@
             1,
             GROUP - 1,
             lambda m, carry: plane(
-                m, lambda v: field[source, v, m - 1], lambda v: field[source, v, m + 1], carry
+                m, lambda: field[source, m - 1], lambda: field[source, m + 1], carry
             ),
             sums,
         )
@@ -320,10 +319,9 @@
 
     def reduce_all(dots, turn):
         tile = jnp.zeros((8, 128), jnp.float32)
-        for d, per_vec in enumerate(dots):
-            for v, value in enumerate(per_vec):
-                whole = jnp.sum(jnp.sum(value, axis=0, keepdims=True), axis=1, keepdims=True)
-                tile = jnp.where((lane == d) & (line == v), whole, tile)
+        for d, value in enumerate(dots):
+            whole = jnp.sum(jnp.sum(value, axis=0, keepdims=True), axis=1, keepdims=True)
+            tile = jnp.where((lane == d) & (line == my_vec), whole, tile)
         for leg, (slots, index, size, target) in enumerate(
             ((part.at[turn], member, GROUP, peer), (part_far.at[turn], group, groups, far))
         ):
@@ -371,15 +369,15 @@
     for k in range(HALF):
         arrive(sent[k])
         if k == 0:
-            rule = lambda v, applied, here, old: applied
+            rule = lambda applied, here, old: applied
         else:
-            rule = lambda v, applied, here, old: 2.0 * applied - old
+            rule = lambda applied, here, old: 2.0 * applied - old
         sums, copies = step(k, k + 1, k - 1 if k else None, k, rule, extra=k == 0)
         sent.append(copies)
         if k == 0:
-            dots[0] = [sums[3 * v + 2] for v in range(vecs)]
-        dots.append([sums[3 * v] for v in range(vecs)])
-        dots.append([sums[3 * v + 1] for v in range(vecs)])
+            dots[0] = sums[2]
+        dots.append(sums[0])
+        dots.append(sums[1])
         if k + 1 <= RETURNED:
             give_back(k + 1)
 
@@ -388,33 +386,37 @@
     arrive(sent[HALF])
     old_at, new_at = HALF + 1, HALF + 2
 
-    def mix(coefficients, v, read):
-        total = coefficients[0][v : v + 1] * read(0)
+    def mix(coefficients, read):
+        total = coefficients[0] * read(0)
         for k in range(1, len(coefficients)):
-            total = total + coefficients[k][v : v + 1] * read(k)
+            total = total + coefficients[k] * read(k)
         return total
 
-    old_mix, new_mix = vectors[HALF - 1][:HALF], vectors[HALF]
+    which = jnp.full((1, lanes), my_vec, jnp.int32)
+
+    def pick(value):
+        row = value[0:1]
+        for v in range(1, vecs):
+            row = jnp.where(which == v, value[v : v + 1], row)
+        return row
+
+    old_mix = [pick(x) for x in vectors[HALF - 1][:HALF]]
+    new_mix = [pick(x) for x in vectors[HALF]]
     for side in range(2):
-        for v in range(vecs):
-            halo[HALF, side, v] = mix(new_mix, v, lambda k: halo[k, side, v])
-
-    def restart(m, sums):
-        sums = list(sums)
-        for v in range(vecs):
-            field[old_at, v, m] = mix(old_mix, v, lambda k: field[k, v, m])
-            new = mix(new_mix, v, lambda k: field[k, v, m])
-            field[new_at, v, m] = new
-            sums[v] = sums[v] + tile_sum(new * new)
-        return tuple(sums)
-
-    sums = lax.fori_loop(0, GROUP, restart, (jnp.zeros((8, lanes), jnp.float32),) * vecs)
-    dots = [list(sums)]
-    gain = 1.0 / offd[HALF - 1]
-    shift = diag[HALF - 1]
-
-    def rule(v, applied, here, old):
-        return gain[v : v + 1] * (applied - shift[v : v + 1] * here) - old
+        halo[HALF, side] = mix(new_mix, lambda k: halo[k, side])
+
+    def restart(m, total):
+        field[old_at, m] = mix(old_mix, lambda k: field[k, m])
+        new = mix(new_mix, lambda k: field[k, m])
+        field[new_at, m] = new
+        return total + tile_sum(new * new)
+
+    dots = [lax.fori_loop(0, GROUP, restart, jnp.zeros((8, lanes), jnp.float32))]
+    gain = pick(1.0 / offd[HALF - 1])
+    shift = pick(diag[HALF - 1])
+
+    def rule(applied, here, old):
+        return gain * (applied - shift * here) - old
 
     for k in range(HALF):
         at = HALF + k
@@ -423,9 +425,9 @@
         last = k == HALF - 1
         sums, copies = step(new_at + k, None if last else new_at + k + 1, new_at + k - 1, at, rule)
         sent.append(copies)
-        dots.append([sums[3 * v] for v in range(vecs)])
+        dots.append(sums[0])
         if not last:
-            dots.append([sums[3 * v + 1] for v in range(vecs)])
+            dots.append(sums[1])
 
     totals = reduce_all(dots, 1)
     diag, offd = phase_two(totals, diag, offd, HALF, jnp.sqrt)
@@ -436,7 +438,7 @@
     for k in range(RETURNED):
         drain(back.at[k], back_recv.at[k])
     for v in range(vecs):
-        cheb[v, 0] = mix(third, v, lambda k: own[v] if k == 0 else back[k - 1, v])
+        cheb[v, 0] = mix([x[v : v + 1] for x in third], lambda k: own[v] if k == 0 else back[k - 1, v])
 
     for ref, items in ((diag_out, diag), (offd_out, offd), (moments_out, moments)):
         at = lax.broadcasted_iota(jnp.int32, ref.shape, 1)
@@ -448,10 +450,10 @@
     for copies in sent:
         for copy in copies:
             copy.wait_send()
-    drain(field.at[0, :, pl.ds(0, GROUP - 1)], vec_sem.at[0])
+    drain(field.at[0, pl.ds(0, GROUP - 1)], vec_sem.at[0])
     drain(level.at[pl.ds(0, GROUP - 1)], level_sem.at[0])
     for k in range(RETURNED):
-        drain(field.at[k + 1, :, pl.ds(0, GROUP - 1), pl.ds(GHOST, rows)], back_send.at[k])
+        drain(field.at[k + 1, pl.ds(0, GROUP - 1), pl.ds(GHOST, rows)], back_send.at[k])
     for turn in range(2):
         drain(part.at[turn, pl.ds(0, GROUP - 1)], red_send.at[turn, 0])
         drain(part_far.at[turn, pl.ds(0, groups - 1)], red_send.at[turn, 1])
@@ -460,7 +462,7 @@
 def shards(count, start_vectors, levels, energies):
     vecs, _, height, lanes = start_vectors.shape
     groups = count // GROUP
-    deep = height // GROUP + 2 * GHOST
+    deep = height // (GROUP // vecs) + 2 * GHOST
     f32 = jnp.float32
     vmem = pl.BlockSpec(memory_space=pltpu.VMEM)
     anywhere = pl.BlockSpec(memory_space=pl.ANY)
@@ -478,8 +480,8 @@
         scratch_shapes=[
             pltpu.VMEM((vecs, height, lanes), f32),
             pltpu.VMEM((height, lanes), jnp.int32),
-            pltpu.VMEM((LANCZOS + 2, vecs, GROUP, deep, lanes), f32),
-            pltpu.VMEM((LANCZOS, 2, vecs, deep, lanes), f32),
+            pltpu.VMEM((LANCZOS + 2, GROUP, deep, lanes), f32),
+            pltpu.VMEM((LANCZOS, 2, deep, lanes), f32),
             pltpu.VMEM((GROUP, deep, lanes), f32),
             pltpu.VMEM((GROUP, deep, lanes), jnp.int32),
             pltpu.VMEM((RETURNED, vecs, height, lanes), f32),
@@ -497,7 +499,7 @@
             dma((2, 2)),
         ],
         compiler_params=pltpu.CompilerParams(
-            collective_id=0, has_side_effects=True, vmem_limit_bytes=48 * 1024 * 1024
+            collective_id=0, has_side_effects=True, vmem_limit_bytes=67043328
         ),
     )(energies, start_vectors, levels)
 

time: 82.6 us -> 76.3 us (0.924)
  Pallas kernels: 76.6 us -> 71.7 us
  local copies, waits for them, and re-layouts: 5.12 us -> 3.76 us
    pallas_call x1, Pallas kernels: 76.6 us -> 71.7 us  [shards(): pl.pallas_call(functools.partial(kernel, count), out_shape=(jax.ShapeDtyp...]
    unnamed x10, local copies, waits for them, and re-layouts: 5.12 us -> 3.76 us
where the time goes in v2:
time: 76.3 us; the launch traced here: 76.1 us
  Pallas kernels  71.7 us (94%)
  local copies, waits for them, and re-layouts  3.76 us (5%)
    pallas_call x1, Pallas kernels, shards(): pl.pallas_call(functools.partial(kernel, count), out_shape=(jax.ShapeDtyp...  71.7 us
    unnamed x10, local copies, waits for them, and re-layouts  3.76 us

profile of v2, /device:TPU:0, one launch (start us, length us, event | category | flops | bytes accessed | tf_op | source)
XLA Modules:
  0.0 76.1 jit_solution(11680691277535913931)
XLA Ops:
  0.6 71.7 %shard_map.66 = (f32[2,1,256,256]{3,2,1,0:T(8,128)}, f32[2,8]{1,0:T(2,128)}, f32[2,7]{1,0:T(2,128)}, f32[2,6]{1,0:T(2,128)}) custom-call(f32[16]{0:T(128)} %energies.1, f32[2,1,256,256]{3,2,1,0:T(8,128)} %start.1, s32[1,256,256]{2,1,0:T(8,128)} %levels.1), custom_call_target="tpu_custom_call" | custom-call | tf_op jit(solution)/shard_map/pallas_call | solution.py:470
  72.3 0.0 copy-start.2
  72.3 1.9 %copy.11 = f32[2,1,256,256]{3,2,1,0:T(8,128)} copy(f32[2,1,256,256]{3,2,1,0:T(8,128)} %get-tuple-element.8) | data formatting | bytes 1048576
  74.2 0.0 copy-done.2
  74.2 0.0 copy-start.1
  74.2 0.6 copy.12
  74.8 0.1 copy-done.1
  74.9 0.0 copy-start
  74.9 0.6 copy.13
  75.4 0.1 copy-done
  75.5 0.6 copy.14
Async XLA Ops:
  72.3 1.9 %copy-start.2 = (f32[2,8]{1,0:T(2,128)S(1)}, f32[2,8]{1,0:T(2,128)}, u32[]{:S(2)}) copy-start(f32[2,8]{1,0:T(2,128)} %get-tuple-element.9) | copy-start | bytes 196
  74.2 0.7 copy-start.1
  74.9 0.7 copy-start

commit v3 on v2

--- a/solution.py
+++ b/solution.py
@@ -241,9 +241,10 @@
     inv_width = 1.0 / width
 
     def halo_copies(slot, at):
+        part_of = pl.ds(GHOST, rows) if at == LANCZOS - 1 else pl.ds(0, deep)
         return [
             pltpu.make_async_remote_copy(
-                src_ref=field.at[slot, plane], dst_ref=halo.at[at, side],
+                src_ref=field.at[slot, plane, part_of], dst_ref=halo.at[at, side, part_of],
                 send_sem=halo_send.at[at, side], recv_sem=halo_recv.at[at, side],
                 device_id=(to,), device_id_type=mesh_id,
             )
@@ -277,39 +278,54 @@
             total = total + x[i : i + 8]
         return total
 
-    def step(source, target, before, at, combine, extra=False):
+    def step(source, target, before, at, combine, awaited, extra=False):
         nothing = jnp.zeros((8, lanes), jnp.float32)
 
-        def plane(m, below, above, sums):
-            sums = list(sums)
-            here = field[source, m]
+        def local(m, here, *beside):
             near = pltpu.roll(here, 1, 0) + pltpu.roll(here, deep - 1, 0)
             near = near + pltpu.roll(here, 1, 1) + pltpu.roll(here, lanes - 1, 1)
-            near = near + below() + above()
-            applied = onsite[m] * here - inv_width * near
+            for plane in beside:
+                near = near + field[source, plane]
+            return onsite[m] * here - inv_width * near
+
+        def finish(m, here, applied):
             new = combine(applied, here, None if before is None else field[before, m])
             if target is not None:
                 field[target, m] = new
+            return new
+
+        def add(sums, here, new):
+            sums = list(sums)
             sums[0] = sums[0] + tile_sum(here * new)
             sums[1] = sums[1] + tile_sum(new * new)
             if extra:
                 sums[2] = sums[2] + tile_sum(here * here)
             return tuple(sums)
 
-        sums = (nothing,) * 3
-        sums = plane(0, lambda: halo[at, 0], lambda: field[source, 1], sums)
-        sums = plane(GROUP - 1, lambda: field[source, GROUP - 2], lambda: halo[at, 1], sums)
+        def plane(m, sums):
+            here = field[source, m]
+            return add(sums, here, finish(m, here, local(m, here, m - 1, m + 1)))
+
+        faces = ((0, 1), (GROUP - 1, GROUP - 2))
+        parts = [local(m, field[source, m], inner) for m, inner in faces]
+        for copy in awaited:
+            copy.wait_recv()
+        news = [
+            finish(m, field[source, m], part - inv_width * halo[at, side])
+            for side, ((m, inner), part) in enumerate(zip(faces, parts))
+        ]
         sent = []
         if target is not None:
             sent = halo_copies(target, at + 1)
             for copy in sent:
                 copy.start()
+        sums = (nothing,) * 3
+        for (m, inner), new in zip(faces, news):
+            sums = add(sums, field[source, m], new)
         sums = lax.fori_loop(
             1,
             GROUP - 1,
-            lambda m, carry: plane(
-                m, lambda: field[source, m - 1], lambda: field[source, m + 1], carry
-            ),
+            plane,
             sums,
         )
         return sums, sent
@@ -367,12 +383,11 @@
 
     dots = [None]
     for k in range(HALF):
-        arrive(sent[k])
         if k == 0:
             rule = lambda applied, here, old: applied
         else:
             rule = lambda applied, here, old: 2.0 * applied - old
-        sums, copies = step(k, k + 1, k - 1 if k else None, k, rule, extra=k == 0)
+        sums, copies = step(k, k + 1, k - 1 if k else None, k, rule, sent[k], extra=k == 0)
         sent.append(copies)
         if k == 0:
             dots[0] = sums[2]
@@ -420,10 +435,8 @@
 
     for k in range(HALF):
         at = HALF + k
-        if k:
-            arrive(sent[at])
         last = k == HALF - 1
-        sums, copies = step(new_at + k, None if last else new_at + k + 1, new_at + k - 1, at, rule)
+        sums, copies = step(new_at + k, None if last else new_at + k + 1, new_at + k - 1, at, rule, sent[at] if k else [])
         sent.append(copies)
         dots.append(sums[0])
         if not last:

time: 76.3 us -> 75.4 us (0.988)
  Pallas kernels: 71.7 us -> 70.8 us
    pallas_call x1, Pallas kernels: 71.7 us -> 70.8 us  [shards(): pl.pallas_call(functools.partial(kernel, count), out_shape=(jax.ShapeDtyp...]
where the time goes in v3:
time: 75.4 us; the launch traced here: 75.3 us
  Pallas kernels  70.8 us (94%)
  local copies, waits for them, and re-layouts  3.76 us (5%)
    pallas_call x1, Pallas kernels, shards(): pl.pallas_call(functools.partial(kernel, count), out_shape=(jax.ShapeDtyp...  70.8 us
    unnamed x10, local copies, waits for them, and re-layouts  3.76 us

profile of v3, /device:TPU:0, one launch (start us, length us, event | category | flops | bytes accessed | tf_op | source)
XLA Modules:
  0.0 75.3 jit_solution(15782984489506941729)
XLA Ops:
  0.6 70.8 %shard_map.66 = (f32[2,1,256,256]{3,2,1,0:T(8,128)}, f32[2,8]{1,0:T(2,128)}, f32[2,7]{1,0:T(2,128)}, f32[2,6]{1,0:T(2,128)}) custom-call(f32[16]{0:T(128)} %energies.1, f32[2,1,256,256]{3,2,1,0:T(8,128)} %start.1, s32[1,256,256]{2,1,0:T(8,128)} %levels.1), custom_call_target="tpu_custom_call" | custom-call | tf_op jit(solution)/shard_map/pallas_call | solution.py:483
  71.5 0.0 copy-start.2
  71.5 1.9 %copy.11 = f32[2,1,256,256]{3,2,1,0:T(8,128)} copy(f32[2,1,256,256]{3,2,1,0:T(8,128)} %get-tuple-element.8) | data formatting | bytes 1048576
  73.4 0.0 copy-done.2
  73.4 0.0 copy-start.1
  73.4 0.6 copy.12
  73.9 0.1 copy-done.1
  74.0 0.0 copy-start
  74.0 0.6 copy.13
  74.6 0.1 copy-done
  74.7 0.6 copy.14
Async XLA Ops:
  71.5 1.9 %copy-start.2 = (f32[2,8]{1,0:T(2,128)S(1)}, f32[2,8]{1,0:T(2,128)}, u32[]{:S(2)}) copy-start(f32[2,8]{1,0:T(2,128)} %get-tuple-element.9) | copy-start | bytes 196
  73.4 0.7 copy-start.1
  74.0 0.7 copy-start

commit v4 on v3

--- a/solution.py
+++ b/solution.py
@@ -327,6 +327,7 @@
             GROUP - 1,
             plane,
             sums,
+            unroll=3,
         )
         return sums, sent
 
@@ -426,7 +427,9 @@
         field[new_at, m] = new
         return total + tile_sum(new * new)
 
-    dots = [lax.fori_loop(0, GROUP, restart, jnp.zeros((8, lanes), jnp.float32))]
+    dots = [
+        lax.fori_loop(0, GROUP, restart, jnp.zeros((8, lanes), jnp.float32), unroll=2)
+    ]
     gain = pick(1.0 / offd[HALF - 1])
     shift = pick(diag[HALF - 1])
 

time: 75.4 us -> 74.7 us (level)
  no operation moved by 1% of the time
where the time goes in v4:
time: 74.7 us; the launch traced here: 74.6 us
  Pallas kernels  70.1 us (94%)
  local copies, waits for them, and re-layouts  3.76 us (5%)
    pallas_call x1, Pallas kernels, shards(): pl.pallas_call(functools.partial(kernel, count), out_shape=(jax.ShapeDtyp...  70.1 us
    unnamed x10, local copies, waits for them, and re-layouts  3.76 us

profile of v4, /device:TPU:0, one launch (start us, length us, event | category | flops | bytes accessed | tf_op | source)
XLA Modules:
  0.0 74.6 jit_solution(9182451934973270311)
XLA Ops:
  0.6 70.1 %shard_map.66 = (f32[2,1,256,256]{3,2,1,0:T(8,128)}, f32[2,8]{1,0:T(2,128)}, f32[2,7]{1,0:T(2,128)}, f32[2,6]{1,0:T(2,128)}) custom-call(f32[16]{0:T(128)} %energies.1, f32[2,1,256,256]{3,2,1,0:T(8,128)} %start.1, s32[1,256,256]{2,1,0:T(8,128)} %levels.1), custom_call_target="tpu_custom_call" | custom-call | tf_op jit(solution)/shard_map/pallas_call | solution.py:486
  70.8 0.0 copy-start.2
  70.8 1.9 %copy.11 = f32[2,1,256,256]{3,2,1,0:T(8,128)} copy(f32[2,1,256,256]{3,2,1,0:T(8,128)} %get-tuple-element.8) | data formatting | bytes 1048576
  72.7 0.0 copy-done.2
  72.7 0.0 copy-start.1
  72.7 0.6 copy.12
  73.2 0.1 copy-done.1
  73.3 0.0 copy-start
  73.3 0.6 copy.13
  73.9 0.1 copy-done
  74.0 0.6 copy.14
Async XLA Ops:
  70.8 1.9 %copy-start.2 = (f32[2,8]{1,0:T(2,128)S(1)}, f32[2,8]{1,0:T(2,128)}, u32[]{:S(2)}) copy-start(f32[2,8]{1,0:T(2,128)} %get-tuple-element.9) | copy-start | bytes 196
  72.7 0.7 copy-start.1
  73.3 0.7 copy-start
